TPU v7x, 32 devices: a whole 2x2x4 slice. The times are simulated.
32 devices in a mesh: group: 2 (over core), node: 4 (over y, x), chip: 4 (over z).
Axes of the slice: x: 2, y: 2, z: 4, core: 2. Of those that a mesh axis runs over, the one named last changes fastest.
Arguments:
- prompt_cache: bfloat16 [2, 4, 4, 96, 576], P('group', 'node', None, 'chip'), may hold values from -4 to 4
- prompt_lengths: int32 [2, 4, 4], replicated, may hold values from 1 to 96, 240 in all within a row
- prompt_replica: int32 [2, 4, 4], replicated, may hold values from 0 to 3, as said below
- new_queries: bfloat16 [2, 4, 4, 2, 128, 576], P('group', 'node', None, None, 'chip'), may hold values from -32 to 32
- new_rows: bfloat16 [2, 4, 4, 2, 576], P('group', 'node'), may hold values from -4 to 4
- resident_cache: bfloat16 [2, 4, 3, 1024, 576], P('group', 'node'), may hold values from -4 to 4
- resident_queries: bfloat16 [2, 4, 3, 2, 128, 576], P('group', 'node', None, None, 'chip'), may hold values from -32 to 32
- resident_rows: bfloat16 [2, 4, 3, 2, 576], P('group', 'node'), may hold values from -4 to 4
- resident_lengths: int32 [2, 4, 3], P('group', 'node'), may hold values from 1 to 1024, 1920 in all within a row
Outputs:
- new_context: bfloat16 [2, 4, 4, 2, 128, 512], P('group', 'node', None, None, 'chip')
- resident_context: bfloat16 [2, 4, 3, 2, 128, 512], P('group', 'node', None, None, 'chip')
Inputs may be any that keep to these rules, and one draw needn't show every extreme that they name: `prompt_replica`: the 4 prompts of one prefill node go to different replicas; one replica may receive prompts from any number of prefill nodes.
All inputs are finite; a program needn't handle non-finite values.
Results may differ from a plain program's by a relative error of at most 0.0034.
Values may be sent and summed in bfloat16 or wider, within the bound.
A program may use at most 64 MiB of HBM per device.

v0:
```python
import functools

import jax
import jax.numpy as jnp
from jax import lax
from jax.experimental import pallas as pl
from jax.experimental.pallas import tpu as pltpu
from jax.sharding import PartitionSpec as P

LATENT = 512
SCALE = 1.0 / 192.0**0.5
RELAY_AT = 1
VMEM_LIMIT = 24 << 20
MESH = pl.DeviceIdType.MESH
NT = (((1,), (1,)), ((), ()))


def dot(a, b, dims=(((1,), (0,)), ((), ()))):
    return lax.dot_general(a, b, dims, preferred_element_type=jnp.float32)


def attend(queries, scores, values, own, step_of_row, finish):
    steps = own.shape[0]
    own32 = own.astype(jnp.float32)
    queries32 = queries.astype(jnp.float32)
    own_scores = []
    for u in range(steps):
        column = jnp.sum(queries32 * own32[u : u + 1], axis=1, keepdims=True) * SCALE
        own_scores.append(jnp.where(step_of_row >= u, column, -jnp.inf))
    top = jnp.max(scores, axis=1, keepdims=True)
    for column in own_scores:
        top = jnp.maximum(top, column)
    weights = jnp.exp(scores - top)
    total = jnp.sum(weights, axis=1, keepdims=True)
    out = values(weights.astype(jnp.bfloat16))
    for u in range(steps):
        weight = jnp.exp(own_scores[u] - top)
        total = total + weight
        out = out + weight.astype(jnp.bfloat16).astype(jnp.float32) * own32[u : u + 1, :LATENT]
    return finish(out, total)


def kernel(
    sizes,
    lengths_hbm,
    replica_hbm,
    resident_lengths_hbm,
    prompt_hbm,
    queries_hbm,
    rows_hbm,
    cache_hbm,
    resident_queries_hbm,
    resident_rows_hbm,
    new_out,
    resident_out,
    lengths_ref,
    replica_ref,
    resident_lengths_ref,
    prompt_ref,
    queries_ref,
    rows_ref,
    cache,
    resident_queries_ref,
    resident_rows_ref,
    stage,
    arrived,
    load_sem,
    cache_sem,
    send_sem,
    relay_sem,
    recv_sem,
):
    groups, nodes, chips = sizes
    group, node, chip = (lax.axis_index(name) for name in ("group", "node", "chip"))
    prompts = prompt_ref.shape[0]
    residents = cache.shape[0]
    steps = rows_ref.shape[1]
    target = lax.rem(group + groups // 2, groups)
    origin = lax.rem(group + groups - groups // 2, groups)
    relayed = False
    direct = tuple(sorted(range(chips), key=lambda k: -min(k, chips - k)))

    barrier = pltpu.get_barrier_semaphore()
    for a in range(nodes):
        for k in direct:
            pl.semaphore_signal(
                barrier,
                inc=1,
                device_id=(origin, lax.rem(node + a, nodes), lax.rem(chip + k, chips)),
                device_id_type=MESH,
            )
    if relayed:
        for k in (1, chips - 1):
            pl.semaphore_signal(
                barrier, inc=1, device_id=(group, node, lax.rem(chip + k, chips)), device_id_type=MESH
            )

    pairs = (
        (replica_hbm, replica_ref),
        (prompt_hbm, prompt_ref),
        (resident_queries_hbm, resident_queries_ref),
        (resident_rows_hbm, resident_rows_ref),
        (resident_lengths_hbm, resident_lengths_ref),
        (queries_hbm, queries_ref),
        (rows_hbm, rows_ref),
        (lengths_hbm, lengths_ref),
    )
    loads = [pltpu.make_async_copy(src, dst, load_sem.at[i]) for i, (src, dst) in enumerate(pairs)]
    cache_loads = [
        pltpu.make_async_copy(cache_hbm.at[r], cache.at[r], cache_sem.at[r])
        for r in range(residents)
    ]
    for load in loads[:5] + cache_loads + loads[5:]:
        load.start()

    loads[0].wait()
    loads[1].wait()
    for a in range(nodes):
        replica = lax.rem(node + a, nodes)
        pick = 0
        for i in range(prompts):
            pick = jnp.where(replica_ref[group, node, i] == replica, i, pick)
        stage[a] = prompt_ref[pick]

    pl.semaphore_wait(barrier, nodes * len(direct) + (2 if relayed else 0))

    def transfer(a, k):
        return pltpu.make_async_remote_copy(
            src_ref=stage.at[a],
            dst_ref=arrived.at[node, chip],
            send_sem=send_sem.at[a, k],
            recv_sem=recv_sem.at[node, chip],
            device_id=(target, lax.rem(node + a, nodes), lax.rem(chip + k, chips)),
            device_id_type=MESH,
        )

    def slot_of(a):
        return lax.rem(node + nodes - a, nodes)

    def relay(a, distance, towards):
        slot = slot_of(a)
        source = lax.rem(chip + chips - towards * distance, chips)
        return pltpu.make_async_remote_copy(
            src_ref=arrived.at[slot, source],
            dst_ref=arrived.at[slot, source],
            send_sem=relay_sem.at[a, distance, (1 - towards) // 2],
            recv_sem=recv_sem.at[slot, source],
            device_id=(group, node, lax.rem(chip + chips + towards, chips)),
            device_id_type=MESH,
        )

    def arrival(slot, source):
        return pltpu.make_async_remote_copy(
            src_ref=stage.at[0],
            dst_ref=arrived.at[slot, source],
            send_sem=send_sem.at[0, 0],
            recv_sem=recv_sem.at[slot, source],
            device_id=(target, node, chip),
            device_id_type=MESH,
        )

    for k in direct:
        for a in reversed(range(nodes)):
            transfer(a, k).start()

    query_rows = queries_ref.shape[1]
    step_of_row = lax.broadcasted_iota(jnp.int32, (query_rows, 1), 0) // (query_rows // steps)

    def reach(a, towards):
        longer = (a % 2 == 0) == (towards > 0)
        return chips // 2 if longer else chips - 1 - chips // 2

    relays = []
    awaited = set()

    def pass_on(distance):
        for a in range(nodes):
            for towards in (1, -1):
                if distance < reach(a, towards):
                    arrival(slot_of(a), lax.rem(chip + chips - towards * distance, chips)).wait_recv()
                    awaited.add((a, towards * distance))
                    copy = relay(a, distance, towards)
                    copy.start()
                    relays.append(copy)

    def resident(r):
        cache_loads[r].wait()
        queries = resident_queries_ref[r]
        scores = dot(queries, cache[r]) * SCALE
        position = lax.broadcasted_iota(jnp.int32, scores.shape, 1)
        scores = jnp.where(position < resident_lengths_ref[r], scores, -jnp.inf)
        resident_out[r] = attend(
            queries,
            scores,
            lambda weights: dot(weights, cache[r, :LATENT], NT),
            resident_rows_ref[r],
            step_of_row,
            lambda out, total: (out / total).astype(resident_out.dtype),
        )

    for load in loads[2:5]:
        load.wait()
    for r in range(residents):
        if relayed and r == min(RELAY_AT, residents - 1):
            pass_on(1)
        resident(r)
    if relayed:
        for distance in range(2, chips // 2):
            pass_on(distance)

    for load in loads[5:]:
        load.wait()
    for a in range(nodes):
        s = slot_of(a)
        length = 0
        live = 0
        for i in range(prompts):
            here = replica_ref[origin, s, i] == node
            length = length + jnp.where(here, lengths_ref[origin, s, i], 0)
            live = live + jnp.where(here, 1, 0)
        offsets = [0]
        for d in range(1, chips):
            offsets.append(d if not relayed or d <= reach(a, 1) else d - chips)
        for d in offsets:
            if (a, d) not in awaited:
                arrival(s, lax.rem(chip + chips - d, chips)).wait_recv()
        tiles = arrived[s].astype(jnp.float32)
        keys = tiles.reshape(-1, tiles.shape[-1]).astype(jnp.bfloat16)
        queries = queries_ref[s]
        scores = dot(queries, keys, NT) * SCALE
        position = lax.broadcasted_iota(jnp.int32, scores.shape, 1)
        scores = jnp.where(position < length, scores, -jnp.inf)
        live32 = jnp.where(live > 0, 1.0, 0.0).astype(jnp.float32)
        new_out[s] = attend(
            queries,
            scores,
            lambda weights, keys=keys: dot(weights, keys[:, :LATENT]),
            rows_ref[s],
            step_of_row,
            lambda out, total, live32=live32: (out / total * live32).astype(new_out.dtype),
        )

    for k in direct:
        for a in range(nodes):
            transfer(a, k).wait_send()
    for copy in relays:
        copy.wait_send()


def write_out(new_ref, resident_ref, new_out, resident_out, sem):
    copies = [
        pltpu.make_async_copy(new_ref, new_out, sem.at[0]),
        pltpu.make_async_copy(resident_ref, resident_out, sem.at[1]),
    ]
    for copy in copies:
        copy.start()
    for copy in copies:
        copy.wait()


def on_device(
    sizes,
    prompt_cache,
    prompt_lengths,
    prompt_replica,
    new_queries,
    new_rows,
    resident_cache,
    resident_queries,
    resident_rows,
    resident_lengths,
):
    groups, nodes, chips = sizes
    prompts, rows, width = prompt_cache.shape[2:]
    residents, length = resident_cache.shape[2:4]
    steps, heads = new_queries.shape[3:5]
    vmem = pl.BlockSpec(memory_space=pltpu.VMEM)
    tiles = (rows // 8, 8, width)
    any_space = pl.BlockSpec(memory_space=pl.ANY)
    outs = (
        jax.ShapeDtypeStruct((nodes, steps * heads, LATENT), jnp.bfloat16),
        jax.ShapeDtypeStruct((residents, steps * heads, LATENT), jnp.bfloat16),
    )
    operands = (
        prompt_lengths,
        prompt_replica,
        resident_lengths.reshape(residents),
        prompt_cache.reshape((prompts,) + tiles),
        new_queries.reshape(nodes, steps * heads, width),
        new_rows.reshape(nodes, steps, width),
        jnp.swapaxes(resident_cache.reshape(residents, length, width), 1, 2),
        resident_queries.reshape(residents, steps * heads, width),
        resident_rows.reshape(residents, steps, width),
    )
    held = [
        (pltpu.VMEM if jnp.issubdtype(x.dtype, jnp.floating) else pltpu.SMEM)(x.shape, x.dtype)
        for x in operands
    ]
    contexts = pl.pallas_call(
        functools.partial(kernel, sizes),
        out_shape=outs,
        in_specs=[pl.BlockSpec(memory_space=pltpu.HBM)] * len(operands),
        out_specs=(vmem, vmem),
        scratch_shapes=held
        + [
            pltpu.VMEM((nodes,) + tiles, jnp.bfloat16),
            pltpu.VMEM((nodes, chips) + tiles, jnp.bfloat16),
            pltpu.SemaphoreType.DMA((len(operands) - 1,)),
            pltpu.SemaphoreType.DMA((residents,)),
            pltpu.SemaphoreType.DMA((nodes, chips)),
            pltpu.SemaphoreType.DMA((nodes, max(2, chips // 2), 2)),
            pltpu.SemaphoreType.DMA((nodes, chips)),
        ],
        compiler_params=pltpu.CompilerParams(
            collective_id=0, has_side_effects=True, vmem_limit_bytes=VMEM_LIMIT
        ),
        name="handoff",
    )(*[pltpu.with_memory_space_constraint(x, pltpu.HBM) for x in operands])
    new_context, resident_context = pl.pallas_call(
        write_out,
        out_shape=outs,
        in_specs=[any_space] * 2,
        out_specs=(pl.BlockSpec(memory_space=pltpu.HBM),) * 2,
        scratch_shapes=[pltpu.SemaphoreType.DMA((2,))],
        compiler_params=pltpu.CompilerParams(vmem_limit_bytes=1 << 20),
        name="write_out",
    )(*contexts)
    return (
        new_context.reshape(1, 1, nodes, steps, heads, LATENT),
        resident_context.reshape(1, 1, residents, steps, heads, LATENT),
    )


def solution(mesh):
    sizes = tuple(mesh.shape[name] for name in ("group", "node", "chip"))
    in_specs = (
        P("group", "node", None, "chip", None),
        P(),
        P(),
        P("group", "node", None, None, "chip", None),
        P("group", "node", None, None, None),
        P("group", "node", None, None, None),
        P("group", "node", None, None, "chip", None),
        P("group", "node", None, None, None),
        P("group", "node", None),
    )
    out_specs = (
        P("group", "node", None, None, "chip", None),
        P("group", "node", None, None, "chip", None),
    )
    return jax.shard_map(
        functools.partial(on_device, sizes),
        mesh=mesh,
        in_specs=in_specs,
        out_specs=out_specs,
        check_vma=False,
    )
```

profile of v0, /device:TPU:9, one launch (start us, length us, event | category | flops | bytes accessed | tf_op | source)
XLA Modules:
  0.0 20.6 jit_solution(150536647685152488)
XLA Ops:
  0.6 19.1 %handoff.1 = (bf16[4,64,512]{2,1,0:T(8,128)(2,1)S(1)}, bf16[3,64,512]{2,1,0:T(8,128)(2,1)S(1)}) custom-call(s32[2,4,4]{2,1,0:T(4,128)} %lengths_hbm.1, s32[2,4,4]{2,1,0:T(4,128)} %replica_hbm.1, s32[3]{0:T(128)} %bitcast.17, bf16[4,3,8,576]{3,2,1,0:T(8,128)(2,1)} %bitcast.14, bf16[4,64,576]{2,1,0:T(8,128)(2,1)} %bitcast.12, bf16[4,2,576]{2,1,0:T(2,128)(2,1)} %bitcast.15, ...), custom_call_target="tpu_custom_call" | custom-call | tf_op jit(solution)/shard_map/handoff/pallas_call | solution.py:299
  19.8 0.8 %write_out.1 = (bf16[4,64,512]{2,1,0:T(8,128)(2,1)}, bf16[3,64,512]{2,1,0:T(8,128)(2,1)}) custom-call(bf16[4,64,512]{2,1,0:T(8,128)(2,1)S(1)} %get-tuple-element.6.new_ref, bf16[3,64,512]{2,1,0:T(8,128)(2,1)S(1)} %get-tuple-element.7.resident_ref), custom_call_target="tpu_custom_call" | custom-call | tf_op jit(solution)/shard_map/write_out/pallas_call | solution.py:319
where the time goes:
time: 20.8 us; the launch traced here: 20.6 us
  Pallas kernels  19.9 us (96%)
  between operations  0.64 us (3%)
    pallas_call x1, Pallas kernels, on_device(): pl.pallas_call(functools.partial(kernel, sizes), out_shape=outs, in_specs...  19.1 us
    pallas_call x1, Pallas kernels, on_device(): pl.pallas_call(write_out, out_shape=outs, in_specs=[any_space] * 2, out_s...  0.78 us

commit v1 on v0

--- a/solution.py
+++ b/solution.py
@@ -9,7 +9,7 @@
 
 LATENT = 512
 SCALE = 1.0 / 192.0**0.5
-RELAY_AT = 1
+REACH = 2
 VMEM_LIMIT = 24 << 20
 MESH = pl.DeviceIdType.MESH
 NT = (((1,), (1,)), ((), ()))
@@ -77,23 +77,56 @@
     steps = rows_ref.shape[1]
     target = lax.rem(group + groups // 2, groups)
     origin = lax.rem(group + groups - groups // 2, groups)
-    relayed = False
-    direct = tuple(sorted(range(chips), key=lambda k: -min(k, chips - k)))
+    xor = nodes & (nodes - 1) == 0
+    order = tuple(reversed(range(nodes)))
+    steps_out = tuple(d for r in range(min(REACH, chips - 1), 0, -1) for d in (r, -r)) + (0,)
+
+    def target_of(a):
+        return node ^ a if xor else lax.rem(node + a, nodes)
+
+    def slot_of(a):
+        return node ^ a if xor else lax.rem(node + nodes - a, nodes)
+
+    def inside(c):
+        return (c >= 0) & (c < chips)
+
+    def direct(source, d):
+        return inside(source + d)
+
+    relay_steps = tuple(
+        (e, towards) for e in range(REACH, chips - 1) for towards in (1, -1)
+    )
+
+    def relays_on(e, towards):
+        return inside(chip - towards * e) & inside(chip + towards)
 
     barrier = pltpu.get_barrier_semaphore()
     for a in range(nodes):
-        for k in direct:
-            pl.semaphore_signal(
-                barrier,
-                inc=1,
-                device_id=(origin, lax.rem(node + a, nodes), lax.rem(chip + k, chips)),
-                device_id_type=MESH,
-            )
-    if relayed:
-        for k in (1, chips - 1):
-            pl.semaphore_signal(
-                barrier, inc=1, device_id=(group, node, lax.rem(chip + k, chips)), device_id_type=MESH
-            )
+        for d in steps_out:
+
+            @pl.when(inside(chip - d))
+            def _(a=a, d=d):
+                pl.semaphore_signal(
+                    barrier,
+                    inc=1,
+                    device_id=(origin, slot_of(a), chip - d),
+                    device_id_type=MESH,
+                )
+
+    expected = 0
+    for d in steps_out:
+        expected = expected + jnp.where(direct(chip, d), nodes, 0)
+    for towards in (1, -1):
+        if any(t == towards for _, t in relay_steps):
+            e = REACH
+
+            @pl.when(inside(chip - towards) & inside(chip - towards - towards * e))
+            def _(towards=towards):
+                pl.semaphore_signal(
+                    barrier, inc=1, device_id=(group, node, chip - towards), device_id_type=MESH
+                )
+
+            expected = expected + jnp.where(relays_on(e, towards), 1, 0)
 
     pairs = (
         (replica_hbm, replica_ref),
@@ -116,36 +149,33 @@
     loads[0].wait()
     loads[1].wait()
     for a in range(nodes):
-        replica = lax.rem(node + a, nodes)
+        replica = target_of(a)
         pick = 0
         for i in range(prompts):
             pick = jnp.where(replica_ref[group, node, i] == replica, i, pick)
         stage[a] = prompt_ref[pick]
 
-    pl.semaphore_wait(barrier, nodes * len(direct) + (2 if relayed else 0))
-
-    def transfer(a, k):
+    pl.semaphore_wait(barrier, expected)
+
+    def transfer(a, d):
         return pltpu.make_async_remote_copy(
             src_ref=stage.at[a],
             dst_ref=arrived.at[node, chip],
-            send_sem=send_sem.at[a, k],
+            send_sem=send_sem.at[a, d + chips - 1],
             recv_sem=recv_sem.at[node, chip],
-            device_id=(target, lax.rem(node + a, nodes), lax.rem(chip + k, chips)),
+            device_id=(target, target_of(a), chip + d),
             device_id_type=MESH,
         )
 
-    def slot_of(a):
-        return lax.rem(node + nodes - a, nodes)
-
-    def relay(a, distance, towards):
+    def relay(a, e, towards):
         slot = slot_of(a)
-        source = lax.rem(chip + chips - towards * distance, chips)
+        source = chip - towards * e
         return pltpu.make_async_remote_copy(
             src_ref=arrived.at[slot, source],
             dst_ref=arrived.at[slot, source],
-            send_sem=relay_sem.at[a, distance, (1 - towards) // 2],
+            send_sem=relay_sem.at[a, e, (1 - towards) // 2],
             recv_sem=recv_sem.at[slot, source],
-            device_id=(group, node, lax.rem(chip + chips + towards, chips)),
+            device_id=(group, node, chip + towards),
             device_id_type=MESH,
         )
 
@@ -159,29 +189,23 @@
             device_id_type=MESH,
         )
 
-    for k in direct:
-        for a in reversed(range(nodes)):
-            transfer(a, k).start()
+    for a in order:
+        for d in steps_out:
+
+            @pl.when(direct(chip, d))
+            def _(a=a, d=d):
+                transfer(a, d).start()
 
     query_rows = queries_ref.shape[1]
     step_of_row = lax.broadcasted_iota(jnp.int32, (query_rows, 1), 0) // (query_rows // steps)
 
-    def reach(a, towards):
-        longer = (a % 2 == 0) == (towards > 0)
-        return chips // 2 if longer else chips - 1 - chips // 2
-
-    relays = []
-    awaited = set()
-
-    def pass_on(distance):
-        for a in range(nodes):
-            for towards in (1, -1):
-                if distance < reach(a, towards):
-                    arrival(slot_of(a), lax.rem(chip + chips - towards * distance, chips)).wait_recv()
-                    awaited.add((a, towards * distance))
-                    copy = relay(a, distance, towards)
-                    copy.start()
-                    relays.append(copy)
+    def pass_on(a):
+        for e, towards in relay_steps:
+
+            @pl.when(relays_on(e, towards))
+            def _(e=e, towards=towards):
+                arrival(slot_of(a), chip - towards * e).wait_recv()
+                relay(a, e, towards).start()
 
     def resident(r):
         cache_loads[r].wait()
@@ -201,16 +225,13 @@
     for load in loads[2:5]:
         load.wait()
     for r in range(residents):
-        if relayed and r == min(RELAY_AT, residents - 1):
-            pass_on(1)
         resident(r)
-    if relayed:
-        for distance in range(2, chips // 2):
-            pass_on(distance)
+    for a in order:
+        pass_on(a)
 
     for load in loads[5:]:
         load.wait()
-    for a in range(nodes):
+    for a in order:
         s = slot_of(a)
         length = 0
         live = 0
@@ -218,12 +239,18 @@
             here = replica_ref[origin, s, i] == node
             length = length + jnp.where(here, lengths_ref[origin, s, i], 0)
             live = live + jnp.where(here, 1, 0)
-        offsets = [0]
-        for d in range(1, chips):
-            offsets.append(d if not relayed or d <= reach(a, 1) else d - chips)
-        for d in offsets:
-            if (a, d) not in awaited:
-                arrival(s, lax.rem(chip + chips - d, chips)).wait_recv()
+        arrival(s, chip).wait_recv()
+        for e in range(1, chips):
+            for towards in (1, -1):
+                source = chip - towards * e
+                here = inside(source)
+                if (e, towards) in relay_steps:
+                    here = here & jnp.logical_not(inside(chip + towards))
+
+                @pl.when(here)
+                def _(s=s, source=source):
+                    arrival(s, source).wait_recv()
+
         tiles = arrived[s].astype(jnp.float32)
         keys = tiles.reshape(-1, tiles.shape[-1]).astype(jnp.bfloat16)
         queries = queries_ref[s]
@@ -240,11 +267,18 @@
             lambda out, total, live32=live32: (out / total * live32).astype(new_out.dtype),
         )
 
-    for k in direct:
-        for a in range(nodes):
-            transfer(a, k).wait_send()
-    for copy in relays:
-        copy.wait_send()
+    for a in order:
+        for d in steps_out:
+
+            @pl.when(direct(chip, d))
+            def _(a=a, d=d):
+                transfer(a, d).wait_send()
+
+        for e, towards in relay_steps:
+
+            @pl.when(relays_on(e, towards))
+            def _(a=a, e=e, towards=towards):
+                relay(a, e, towards).wait_send()
 
 
 def write_out(new_ref, resident_ref, new_out, resident_out, sem):
@@ -307,8 +341,8 @@
             pltpu.VMEM((nodes, chips) + tiles, jnp.bfloat16),
             pltpu.SemaphoreType.DMA((len(operands) - 1,)),
             pltpu.SemaphoreType.DMA((residents,)),
-            pltpu.SemaphoreType.DMA((nodes, chips)),
-            pltpu.SemaphoreType.DMA((nodes, max(2, chips // 2), 2)),
+            pltpu.SemaphoreType.DMA((nodes, 2 * chips - 1)),
+            pltpu.SemaphoreType.DMA((nodes, chips, 2)),
             pltpu.SemaphoreType.DMA((nodes, chips)),
         ],
         compiler_params=pltpu.CompilerParams(

time: 20.8 us -> 19.4 us (0.933)
  the two profiles are of different devices: /device:TPU:9 before, /device:TPU:0 now
where the time goes in v1:
time: 19.4 us; the launch traced here: 19.2 us
  Pallas kernels  18.5 us (95%)
  between operations  0.64 us (3%)
    pallas_call x1, Pallas kernels, on_device(): pl.pallas_call(functools.partial(kernel, sizes), out_shape=outs, in_specs...  17.8 us
    pallas_call x1, Pallas kernels, on_device(): pl.pallas_call(write_out, out_shape=outs, in_specs=[any_space] * 2, out_s...  0.78 us

profile of v1, /device:TPU:0, one launch (start us, length us, event | category | flops | bytes accessed | tf_op | source)
XLA Modules:
  0.0 19.2 jit_solution(5498663014301685736)
XLA Ops:
  0.6 17.8 %handoff.1 = (bf16[4,64,512]{2,1,0:T(8,128)(2,1)S(1)}, bf16[3,64,512]{2,1,0:T(8,128)(2,1)S(1)}) custom-call(s32[2,4,4]{2,1,0:T(4,128)} %lengths_hbm.1, s32[2,4,4]{2,1,0:T(4,128)} %replica_hbm.1, s32[3]{0:T(128)} %bitcast.17, bf16[4,3,8,576]{3,2,1,0:T(8,128)(2,1)} %bitcast.14, bf16[4,64,576]{2,1,0:T(8,128)(2,1)} %bitcast.12, bf16[4,2,576]{2,1,0:T(2,128)(2,1)} %bitcast.15, ...), custom_call_target="tpu_custom_call" | custom-call | tf_op jit(solution)/shard_map/handoff/pallas_call | solution.py:333
  18.4 0.8 %write_out.1 = (bf16[4,64,512]{2,1,0:T(8,128)(2,1)}, bf16[3,64,512]{2,1,0:T(8,128)(2,1)}) custom-call(bf16[4,64,512]{2,1,0:T(8,128)(2,1)S(1)} %get-tuple-element.6.new_ref, bf16[3,64,512]{2,1,0:T(8,128)(2,1)S(1)} %get-tuple-element.7.resident_ref), custom_call_target="tpu_custom_call" | custom-call | tf_op jit(solution)/shard_map/write_out/pallas_call | solution.py:353

commit v2 on v1

--- a/solution.py
+++ b/solution.py
@@ -8,8 +8,8 @@
 from jax.sharding import PartitionSpec as P
 
 LATENT = 512
+LANES = 128
 SCALE = 1.0 / 192.0**0.5
-REACH = 2
 VMEM_LIMIT = 24 << 20
 MESH = pl.DeviceIdType.MESH
 NT = (((1,), (1,)), ((), ()))
@@ -38,6 +38,43 @@
         total = total + weight
         out = out + weight.astype(jnp.bfloat16).astype(jnp.float32) * own32[u : u + 1, :LATENT]
     return finish(out, total)
+
+
+def tile_counts(bands, width):
+    across = LATENT // LANES
+    share = LANES // (width - LATENT)
+    return across, share, bands * across + -(-bands // share)
+
+
+def pack(prompt_ref, pick, stage, a):
+    bands, band, width = prompt_ref.shape[1:]
+    across, share, count = tile_counts(bands, width)
+    for g in range(bands):
+        for c in range(across):
+            stage[a, g * across + c] = prompt_ref[pick, g, :, c * LANES : (c + 1) * LANES]
+    for i in range(count - bands * across):
+        tails = [
+            prompt_ref[pick, g, :, LATENT:width].astype(jnp.float32)
+            for g in range(i * share, min(bands, (i + 1) * share))
+        ]
+        tails += [jnp.zeros_like(tails[0])] * (share - len(tails))
+        stage[a, bands * across + i] = jnp.concatenate(tails, axis=1).astype(stage.dtype)
+
+
+def unpack(tiles, bands, band, width):
+    across, share, count = tile_counts(bands, width)
+    chips = tiles.shape[0]
+    rows = chips * bands * band
+    latent = tiles[:, : bands * across].reshape(chips, bands, across, band, LANES)
+    columns = [latent[:, :, c].reshape(rows, LANES) for c in range(across)]
+    tails = []
+    for k in range(chips):
+        for g in range(bands):
+            tile = tiles[k, bands * across + g // share]
+            at = g % share * (width - LATENT)
+            tails.append(pltpu.roll(tile, LANES - at, 1) if at else tile)
+    columns.append(jnp.concatenate(tails, axis=0)[:, : width - LATENT])
+    return jnp.concatenate(columns, axis=1).astype(jnp.bfloat16)
 
 
 def kernel(
@@ -69,6 +106,7 @@
     send_sem,
     relay_sem,
     recv_sem,
+    ready,
 ):
     groups, nodes, chips = sizes
     group, node, chip = (lax.axis_index(name) for name in ("group", "node", "chip"))
@@ -79,54 +117,64 @@
     origin = lax.rem(group + groups - groups // 2, groups)
     xor = nodes & (nodes - 1) == 0
     order = tuple(reversed(range(nodes)))
-    steps_out = tuple(d for r in range(min(REACH, chips - 1), 0, -1) for d in (r, -r)) + (0,)
-
     def target_of(a):
         return node ^ a if xor else lax.rem(node + a, nodes)
 
     def slot_of(a):
         return node ^ a if xor else lax.rem(node + nodes - a, nodes)
 
-    def inside(c):
-        return (c >= 0) & (c < chips)
-
-    def direct(source, d):
-        return inside(source + d)
-
-    relay_steps = tuple(
-        (e, towards) for e in range(REACH, chips - 1) for towards in (1, -1)
-    )
-
-    def relays_on(e, towards):
-        return inside(chip - towards * e) & inside(chip + towards)
-
+    line = range(chips)
+
+    def direct(s, t):
+        return abs(t - s) <= 2 if s > t else abs(t - s) == 1 or s == 0
+
+    def relays_of(c):
+        found = [(s, 1) for s in line[: c + 1] if c + 1 < chips and not direct(s, c + 1)]
+        return found + [(s, -1) for s in line[c:] if c > 0 and not direct(s, c - 1)]
+
+    def sends_of(c):
+        return [t - c for t in line if t != c and direct(c, t)]
+
+    def at_chip(body):
+        for c in line:
+            pl.when(chip == c)(functools.partial(body, c))
+
+    def linked(low, high):
+        return direct(low, high) or direct(high, low)
+
+    def relay_link(low):
+        up = any(way == 1 for _, way in relays_of(low))
+        return up or any(way == -1 for _, way in relays_of(low + 1))
+
+    peers = (target,) if groups % 2 == 0 else (target, origin)
     barrier = pltpu.get_barrier_semaphore()
-    for a in range(nodes):
-        for d in steps_out:
-
-            @pl.when(inside(chip - d))
-            def _(a=a, d=d):
-                pl.semaphore_signal(
-                    barrier,
-                    inc=1,
-                    device_id=(origin, slot_of(a), chip - d),
-                    device_id_type=MESH,
-                )
-
-    expected = 0
-    for d in steps_out:
-        expected = expected + jnp.where(direct(chip, d), nodes, 0)
-    for towards in (1, -1):
-        if any(t == towards for _, t in relay_steps):
-            e = REACH
-
-            @pl.when(inside(chip - towards) & inside(chip - towards - towards * e))
-            def _(towards=towards):
-                pl.semaphore_signal(
-                    barrier, inc=1, device_id=(group, node, chip - towards), device_id_type=MESH
-                )
-
-            expected = expected + jnp.where(relays_on(e, towards), 1, 0)
+
+    def tell(sem, to):
+        pl.semaphore_signal(sem, inc=1, device_id=to, device_id_type=MESH)
+
+    def enter(c):
+        for high in reversed(line[c + 1 :]):
+            if linked(c, high):
+                for peer in peers:
+                    for a in order:
+                        tell(barrier, (peer, slot_of(a), high))
+        if c + 1 < chips and relay_link(c):
+            tell(barrier, (group, node, c + 1))
+        for a in order:
+            tell(barrier, (origin, slot_of(a), c))
+
+    def entered(c):
+        expected = nodes + nodes * len(peers) * sum(linked(low, c) for low in line[:c])
+        expected += 1 if c > 0 and relay_link(c - 1) else 0
+        pl.semaphore_wait(barrier, expected)
+        for low in line[:c]:
+            if direct(low, c):
+                for a in order:
+                    tell(ready.at[c - low], (origin, slot_of(a), low))
+        if c > 0 and any(way == 1 for _, way in relays_of(c - 1)):
+            tell(ready.at[0], (group, node, c - 1))
+
+    at_chip(enter)
 
     pairs = (
         (replica_hbm, replica_ref),
@@ -146,6 +194,7 @@
     for load in loads[:5] + cache_loads + loads[5:]:
         load.start()
 
+    at_chip(entered)
     loads[0].wait()
     loads[1].wait()
     for a in range(nodes):
@@ -153,9 +202,7 @@
         pick = 0
         for i in range(prompts):
             pick = jnp.where(replica_ref[group, node, i] == replica, i, pick)
-        stage[a] = prompt_ref[pick]
-
-    pl.semaphore_wait(barrier, expected)
+        pack(prompt_ref, pick, stage, a)
 
     def transfer(a, d):
         return pltpu.make_async_remote_copy(
@@ -167,15 +214,14 @@
             device_id_type=MESH,
         )
 
-    def relay(a, e, towards):
+    def relay(a, source, way):
         slot = slot_of(a)
-        source = chip - towards * e
         return pltpu.make_async_remote_copy(
             src_ref=arrived.at[slot, source],
             dst_ref=arrived.at[slot, source],
-            send_sem=relay_sem.at[a, e, (1 - towards) // 2],
+            send_sem=relay_sem.at[a, source],
             recv_sem=recv_sem.at[slot, source],
-            device_id=(group, node, chip + towards),
+            device_id=(group, node, chip + way),
             device_id_type=MESH,
         )
 
@@ -189,23 +235,38 @@
             device_id_type=MESH,
         )
 
-    for a in order:
-        for d in steps_out:
-
-            @pl.when(direct(chip, d))
-            def _(a=a, d=d):
+    def later(c, d):
+        return c == chips - 2 and d == -1
+
+    def send(c):
+        for d in sorted(d for d in sends_of(c) if d < 0 and not later(c, d)):
+            for a in order:
                 transfer(a, d).start()
+        for a in order:
+            transfer(a, 0).start()
+        for d in [d for d in sends_of(c) if d > 0]:
+            pl.semaphore_wait(ready.at[d], nodes)
+            for a in order:
+                transfer(a, d).start()
+
+    def send_later(c):
+        for d in sends_of(c):
+            if later(c, d):
+                for a in order:
+                    transfer(a, d).start()
+
+    at_chip(send)
 
     query_rows = queries_ref.shape[1]
     step_of_row = lax.broadcasted_iota(jnp.int32, (query_rows, 1), 0) // (query_rows // steps)
 
-    def pass_on(a):
-        for e, towards in relay_steps:
-
-            @pl.when(relays_on(e, towards))
-            def _(e=e, towards=towards):
-                arrival(slot_of(a), chip - towards * e).wait_recv()
-                relay(a, e, towards).start()
+    def pass_on(c):
+        if any(way == 1 for _, way in relays_of(c)):
+            pl.semaphore_wait(ready.at[0], 1)
+        for a in order:
+            for source, way in relays_of(c):
+                arrival(slot_of(a), source).wait_recv()
+                relay(a, source, way).start()
 
     def resident(r):
         cache_loads[r].wait()
@@ -226,8 +287,9 @@
         load.wait()
     for r in range(residents):
         resident(r)
-    for a in order:
-        pass_on(a)
+        if r == 1:
+            at_chip(send_later)
+    at_chip(pass_on)
 
     for load in loads[5:]:
         load.wait()
@@ -239,20 +301,15 @@
             here = replica_ref[origin, s, i] == node
             length = length + jnp.where(here, lengths_ref[origin, s, i], 0)
             live = live + jnp.where(here, 1, 0)
-        arrival(s, chip).wait_recv()
-        for e in range(1, chips):
-            for towards in (1, -1):
-                source = chip - towards * e
-                here = inside(source)
-                if (e, towards) in relay_steps:
-                    here = here & jnp.logical_not(inside(chip + towards))
-
-                @pl.when(here)
-                def _(s=s, source=source):
+
+        def settle(c, s=s):
+            passed = [source for source, _ in relays_of(c)]
+            for source in line:
+                if source not in passed:
                     arrival(s, source).wait_recv()
 
-        tiles = arrived[s].astype(jnp.float32)
-        keys = tiles.reshape(-1, tiles.shape[-1]).astype(jnp.bfloat16)
+        at_chip(settle)
+        keys = unpack(arrived[s].astype(jnp.float32), *prompt_ref.shape[1:])
         queries = queries_ref[s]
         scores = dot(queries, keys, NT) * SCALE
         position = lax.broadcasted_iota(jnp.int32, scores.shape, 1)
@@ -267,18 +324,14 @@
             lambda out, total, live32=live32: (out / total * live32).astype(new_out.dtype),
         )
 
-    for a in order:
-        for d in steps_out:
-
-            @pl.when(direct(chip, d))
-            def _(a=a, d=d):
+    def drain(c):
+        for a in order:
+            for d in sends_of(c) + [0]:
                 transfer(a, d).wait_send()
-
-        for e, towards in relay_steps:
-
-            @pl.when(relays_on(e, towards))
-            def _(a=a, e=e, towards=towards):
-                relay(a, e, towards).wait_send()
+            for source, way in relays_of(c):
+                relay(a, source, way).wait_send()
+
+    at_chip(drain)
 
 
 def write_out(new_ref, resident_ref, new_out, resident_out, sem):
@@ -310,6 +363,7 @@
     steps, heads = new_queries.shape[3:5]
     vmem = pl.BlockSpec(memory_space=pltpu.VMEM)
     tiles = (rows // 8, 8, width)
+    packed = (tile_counts(rows // 8, width)[2], 8, LANES)
     any_space = pl.BlockSpec(memory_space=pl.ANY)
     outs = (
         jax.ShapeDtypeStruct((nodes, steps * heads, LATENT), jnp.bfloat16),
@@ -337,13 +391,14 @@
         out_specs=(vmem, vmem),
         scratch_shapes=held
         + [
-            pltpu.VMEM((nodes,) + tiles, jnp.bfloat16),
-            pltpu.VMEM((nodes, chips) + tiles, jnp.bfloat16),
+            pltpu.VMEM((nodes,) + packed, jnp.bfloat16),
+            pltpu.VMEM((nodes, chips) + packed, jnp.bfloat16),
             pltpu.SemaphoreType.DMA((len(operands) - 1,)),
             pltpu.SemaphoreType.DMA((residents,)),
             pltpu.SemaphoreType.DMA((nodes, 2 * chips - 1)),
-            pltpu.SemaphoreType.DMA((nodes, chips, 2)),
             pltpu.SemaphoreType.DMA((nodes, chips)),
+            pltpu.SemaphoreType.DMA((nodes, chips)),
+            pltpu.SemaphoreType.REGULAR((chips,)),
         ],
         compiler_params=pltpu.CompilerParams(
             collective_id=0, has_side_effects=True, vmem_limit_bytes=VMEM_LIMIT

time: 19.4 us -> 17.7 us (0.912)
  Pallas kernels: 18.5 us -> 17 us
    pallas_call x1, Pallas kernels: 17.8 us -> 16.2 us  [on_device(): pl.pallas_call(functools.partial(kernel, sizes), out_shape=outs, in_specs...]
where the time goes in v2:
time: 17.7 us; the launch traced here: 17.6 us
  Pallas kernels  17 us (96%)
  between operations  0.64 us (4%)
    pallas_call x1, Pallas kernels, on_device(): pl.pallas_call(functools.partial(kernel, sizes), out_shape=outs, in_specs...  16.2 us
    pallas_call x1, Pallas kernels, on_device(): pl.pallas_call(write_out, out_shape=outs, in_specs=[any_space] * 2, out_s...  0.78 us

profile of v2, /device:TPU:0, one launch (start us, length us, event | category | flops | bytes accessed | tf_op | source)
XLA Modules:
  0.0 17.6 jit_solution(13791838338404048460)
XLA Ops:
  0.6 16.2 %handoff.1 = (bf16[4,64,512]{2,1,0:T(8,128)(2,1)S(1)}, bf16[3,64,512]{2,1,0:T(8,128)(2,1)S(1)}) custom-call(s32[2,4,4]{2,1,0:T(4,128)} %lengths_hbm.1, s32[2,4,4]{2,1,0:T(4,128)} %replica_hbm.1, s32[3]{0:T(128)} %bitcast.17, bf16[4,3,8,576]{3,2,1,0:T(8,128)(2,1)} %bitcast.14, bf16[4,64,576]{2,1,0:T(8,128)(2,1)} %bitcast.12, bf16[4,2,576]{2,1,0:T(2,128)(2,1)} %bitcast.15, ...), custom_call_target="tpu_custom_call" | custom-call | tf_op jit(solution)/shard_map/handoff/pallas_call | solution.py:387
  16.8 0.8 %write_out.1 = (bf16[4,64,512]{2,1,0:T(8,128)(2,1)}, bf16[3,64,512]{2,1,0:T(8,128)(2,1)}) custom-call(bf16[4,64,512]{2,1,0:T(8,128)(2,1)S(1)} %get-tuple-element.6.new_ref, bf16[3,64,512]{2,1,0:T(8,128)(2,1)S(1)} %get-tuple-element.7.resident_ref), custom_call_target="tpu_custom_call" | custom-call | tf_op jit(solution)/shard_map/write_out/pallas_call | solution.py:408

commit v3 on v2

--- a/solution.py
+++ b/solution.py
@@ -107,6 +107,7 @@
     relay_sem,
     recv_sem,
     ready,
+    plane,
 ):
     groups, nodes, chips = sizes
     group, node, chip = (lax.axis_index(name) for name in ("group", "node", "chip"))
@@ -116,35 +117,38 @@
     target = lax.rem(group + groups // 2, groups)
     origin = lax.rem(group + groups - groups // 2, groups)
     xor = nodes & (nodes - 1) == 0
-    order = tuple(reversed(range(nodes)))
+    order = tuple(range(nodes))
     def target_of(a):
         return node ^ a if xor else lax.rem(node + a, nodes)
 
     def slot_of(a):
         return node ^ a if xor else lax.rem(node + nodes - a, nodes)
 
+    split = xor and groups % 2 == 0
     line = range(chips)
 
-    def direct(s, t):
-        return abs(t - s) <= 2 if s > t else abs(t - s) == 1 or s == 0
-
-    def relays_of(c):
-        found = [(s, 1) for s in line[: c + 1] if c + 1 < chips and not direct(s, c + 1)]
-        return found + [(s, -1) for s in line[c:] if c > 0 and not direct(s, c - 1)]
-
-    def sends_of(c):
-        return [t - c for t in line if t != c and direct(c, t)]
+    def direct(s, t, a):
+        return abs(t - s) <= 2 if s > t else (abs(t - s) == 1 or s == 0)
+
+    def relays_of(c, a):
+        found = [(s, 1) for s in line[: c + 1] if c + 1 < chips and not direct(s, c + 1, a)]
+        return found + [(s, -1) for s in line[c:] if c > 0 and not direct(s, c - 1, a)]
+
+    def relays_any(c, way):
+        return any(w == way for a in order for _, w in relays_of(c, a))
+
+    def sends_of(c, a):
+        return [t - c for t in line if t != c and direct(c, t, a)]
 
     def at_chip(body):
         for c in line:
             pl.when(chip == c)(functools.partial(body, c))
 
     def linked(low, high):
-        return direct(low, high) or direct(high, low)
+        return any(direct(low, high, a) or direct(high, low, a) for a in order)
 
     def relay_link(low):
-        up = any(way == 1 for _, way in relays_of(low))
-        return up or any(way == -1 for _, way in relays_of(low + 1))
+        return relays_any(low, 1) or relays_any(low + 1, -1)
 
     peers = (target,) if groups % 2 == 0 else (target, origin)
     barrier = pltpu.get_barrier_semaphore()
@@ -161,17 +165,27 @@
         if c + 1 < chips and relay_link(c):
             tell(barrier, (group, node, c + 1))
         for a in order:
-            tell(barrier, (origin, slot_of(a), c))
+            if split and a > 0:
+                pl.when(slot_of(a) > node)(
+                    functools.partial(tell, barrier, (origin, slot_of(a), c))
+                )
+            else:
+                tell(barrier, (origin, slot_of(a), c))
 
     def entered(c):
-        expected = nodes + nodes * len(peers) * sum(linked(low, c) for low in line[:c])
+        expected = (node + 1 if split else nodes) + nodes * len(peers) * sum(linked(low, c) for low in line[:c])
         expected += 1 if c > 0 and relay_link(c - 1) else 0
         pl.semaphore_wait(barrier, expected)
         for low in line[:c]:
-            if direct(low, c):
-                for a in order:
+            for a in order:
+                if direct(low, c, a):
                     tell(ready.at[c - low], (origin, slot_of(a), low))
-        if c > 0 and any(way == 1 for _, way in relays_of(c - 1)):
+        if split:
+            for a in order[1:]:
+                pl.when(slot_of(a) < node)(
+                    functools.partial(tell, plane.at[a], (origin, slot_of(a), c))
+                )
+        if c > 0 and relays_any(c - 1, 1):
             tell(ready.at[0], (group, node, c - 1))
 
     at_chip(enter)
@@ -239,20 +253,34 @@
         return c == chips - 2 and d == -1
 
     def send(c):
-        for d in sorted(d for d in sends_of(c) if d < 0 and not later(c, d)):
+        for d in range(-c, 0):
             for a in order:
+                if d in sends_of(c, a) and not later(c, d):
+                    transfer(a, d).start()
+        for a in order:
+            if split and a > 0:
+                pl.when(target_of(a) < node)(transfer(a, 0).start)
+            else:
+                transfer(a, 0).start()
+
+        def acknowledged(a):
+            pl.semaphore_wait(plane.at[a], 1)
+            transfer(a, 0).start()
+
+        if split:
+            for a in range(1, nodes):
+                pl.when(target_of(a) > node)(functools.partial(acknowledged, a))
+        for d in range(1, chips - c):
+            using = [a for a in order if d in sends_of(c, a)]
+            if using:
+                pl.semaphore_wait(ready.at[d], len(using))
+            for a in using:
                 transfer(a, d).start()
-        for a in order:
-            transfer(a, 0).start()
-        for d in [d for d in sends_of(c) if d > 0]:
-            pl.semaphore_wait(ready.at[d], nodes)
+
+    def send_later(c):
+        for d in range(-c, 0):
             for a in order:
-                transfer(a, d).start()
-
-    def send_later(c):
-        for d in sends_of(c):
-            if later(c, d):
-                for a in order:
+                if d in sends_of(c, a) and later(c, d):
                     transfer(a, d).start()
 
     at_chip(send)
@@ -261,10 +289,10 @@
     step_of_row = lax.broadcasted_iota(jnp.int32, (query_rows, 1), 0) // (query_rows // steps)
 
     def pass_on(c):
-        if any(way == 1 for _, way in relays_of(c)):
+        if relays_any(c, 1):
             pl.semaphore_wait(ready.at[0], 1)
         for a in order:
-            for source, way in relays_of(c):
+            for source, way in relays_of(c, a):
                 arrival(slot_of(a), source).wait_recv()
                 relay(a, source, way).start()
 
@@ -302,8 +330,8 @@
             length = length + jnp.where(here, lengths_ref[origin, s, i], 0)
             live = live + jnp.where(here, 1, 0)
 
-        def settle(c, s=s):
-            passed = [source for source, _ in relays_of(c)]
+        def settle(c, s=s, a=a):
+            passed = [source for source, _ in relays_of(c, a)]
             for source in line:
                 if source not in passed:
                     arrival(s, source).wait_recv()
@@ -326,9 +354,9 @@
 
     def drain(c):
         for a in order:
-            for d in sends_of(c) + [0]:
+            for d in sends_of(c, a) + [0]:
                 transfer(a, d).wait_send()
-            for source, way in relays_of(c):
+            for source, way in relays_of(c, a):
                 relay(a, source, way).wait_send()
 
     at_chip(drain)
@@ -399,6 +427,7 @@
             pltpu.SemaphoreType.DMA((nodes, chips)),
             pltpu.SemaphoreType.DMA((nodes, chips)),
             pltpu.SemaphoreType.REGULAR((chips,)),
+            pltpu.SemaphoreType.REGULAR((nodes,)),
         ],
         compiler_params=pltpu.CompilerParams(
             collective_id=0, has_side_effects=True, vmem_limit_bytes=VMEM_LIMIT

time: 17.7 us -> 17.6 us (level)
  Pallas kernels: 17 us -> 16.8 us
where the time goes in v3:
time: 17.6 us; the launch traced here: 17.5 us
  Pallas kernels  16.8 us (95%)
  between operations  0.64 us (4%)
    pallas_call x1, Pallas kernels, on_device(): pl.pallas_call(functools.partial(kernel, sizes), out_shape=outs, in_specs...  16 us
    pallas_call x1, Pallas kernels, on_device(): pl.pallas_call(write_out, out_shape=outs, in_specs=[any_space] * 2, out_s...  0.78 us

profile of v3, /device:TPU:0, one launch (start us, length us, event | category | flops | bytes accessed | tf_op | source)
XLA Modules:
  0.0 17.5 jit_solution(15960612919240565091)
XLA Ops:
  0.6 16.0 %handoff.1 = (bf16[4,64,512]{2,1,0:T(8,128)(2,1)S(1)}, bf16[3,64,512]{2,1,0:T(8,128)(2,1)S(1)}) custom-call(s32[2,4,4]{2,1,0:T(4,128)} %lengths_hbm.1, s32[2,4,4]{2,1,0:T(4,128)} %replica_hbm.1, s32[3]{0:T(128)} %bitcast.17, bf16[4,3,8,576]{3,2,1,0:T(8,128)(2,1)} %bitcast.14, bf16[4,64,576]{2,1,0:T(8,128)(2,1)} %bitcast.12, bf16[4,2,576]{2,1,0:T(2,128)(2,1)} %bitcast.15, ...), custom_call_target="tpu_custom_call" | custom-call | tf_op jit(solution)/shard_map/handoff/pallas_call | solution.py:415
  16.7 0.8 %write_out.1 = (bf16[4,64,512]{2,1,0:T(8,128)(2,1)}, bf16[3,64,512]{2,1,0:T(8,128)(2,1)}) custom-call(bf16[4,64,512]{2,1,0:T(8,128)(2,1)S(1)} %get-tuple-element.6.new_ref, bf16[3,64,512]{2,1,0:T(8,128)(2,1)S(1)} %get-tuple-element.7.resident_ref), custom_call_target="tpu_custom_call" | custom-call | tf_op jit(solution)/shard_map/write_out/pallas_call | solution.py:437
